TPU v7x, 32 devices: a whole 2x2x4 slice. The times are simulated.
32 devices in a mesh: groups: 2 (over y), pts: 4 (over z), cb: 4 (over x, core).
Axes of the slice: x: 2, y: 2, z: 4, core: 2. Of those that a mesh axis runs over, the one named last changes fastest.
Arguments:
- points: bfloat16 [16384, 768], P(('groups', 'pts')), parts along dimension 0, may hold values from -60 to 60
- code_one: int32 [16384], P(('groups', 'pts')), parts along dimension 0, may hold values from 0 to 2047
- code_two: int32 [16384], P(('groups', 'pts')), parts along dimension 0, may hold values from 0 to 2047
- cent_one: bfloat16 [4096, 768], P(('groups', 'cb')), parts along dimension 0, may hold values from -6 to 6
- cent_two: bfloat16 [4096, 768], P(('groups', 'cb')), parts along dimension 0, may hold values from -6 to 6
Outputs:
- new_one: bfloat16 [4096, 768], P(('groups', 'cb')), parts along dimension 0
- new_two: bfloat16 [4096, 768], P(('groups', 'cb')), parts along dimension 0
- distortion: float32 [4], P('groups'), parts along dimension 0
There are 2 independent parts, one for each index of `groups`. A program takes and returns all parts, laid end to end along the dimension named above; each array names one. Nothing has to cross between parts.
All inputs are finite; a program needn't handle non-finite values.
Results may differ from a plain program's by a relative error of at most 0.0014.
Values may be sent and summed in bfloat16 or wider, within the bound.
A program may use at most 64 MiB of HBM per device.

v0:
```python
import functools

import jax
import jax.numpy as jnp
from jax import lax
from jax.experimental import pallas as pl
from jax.experimental.pallas import tpu as pltpu
from jax.sharding import PartitionSpec as P

F32 = jnp.float32
BF16 = jnp.bfloat16
CORES = 2
PARTS = 8
LAG = 3
WINDOW = 2


def fused_kernel(
    npts, ncb, parts, lag, window,
    points, code_one, code_two, cent_one, cent_two,
    new_one, new_two, total_out,
    residual, codebook, sums, from_left, from_right, codes_all, mins, mins_in, tot, tot_in,
    scaled, csq, squares,
    rs_send, rs_recv, ag_send, ag_recv,
    x_send, x_recv, d_send, d_recv, code_send, code_recv, min_send, min_recv, tot_send, tot_recv,
):
    p = lax.axis_index("pts")
    c = lax.axis_index("cb")
    last = npts - 1
    npoints, width = points.shape
    rows = cent_one.shape[0]
    size = rows // (2 * parts)
    ids = rows * ncb
    nx = ncb // CORES
    cx, cc = c // CORES, c % CORES
    sibling = cx * CORES + (1 - cc)

    def to(axis, src, dst, s, r, where):
        return pltpu.make_async_remote_copy(
            src_ref=src, dst_ref=dst, send_sem=s, recv_sem=r,
            device_id={axis: where}, device_id_type=pl.DeviceIdType.MESH,
        )

    barrier = pltpu.get_barrier_semaphore()
    for d in range(1, npts):
        pl.semaphore_signal(barrier, inc=1, device_id={"pts": (p + d) % npts},
                            device_id_type=pl.DeviceIdType.MESH)
    for d in range(1, ncb):
        pl.semaphore_signal(barrier, inc=1, device_id={"cb": (c + d) % ncb},
                            device_id_type=pl.DeviceIdType.MESH)

    span = rows // npts

    def partial_sums(data, code):
        def one(t, carry):
            label = c * rows + t * span + lax.broadcasted_iota(jnp.int32, (span, npoints), 0)
            onehot = jnp.where(code[...] == label, 1.0, 0.0).astype(BF16)
            at = pl.ds(pl.multiple_of(t * span, span), span)
            sums[at, :] = jnp.dot(onehot, data[...], preferred_element_type=F32)
            return carry

        lax.fori_loop(0, npts, one, 0)

    def code_copy(k, d, slot):
        code = (code_one, code_two)[k]
        return to("pts", code, codes_all.at[k, slot], code_send.at[k, d], code_recv.at[k, d],
                  (p + d) % npts)

    def part(g):
        return pl.ds(pl.multiple_of(g * size, size), size)

    def count(k, g):
        label = c * rows + g * size + lax.broadcasted_iota(jnp.int32, (size, npoints), 0)
        acc = jnp.zeros((size, npoints), F32)
        for t in range(npts):
            acc = acc + jnp.where(codes_all[k, t] == label, 1.0, 0.0)
        return jnp.sum(acc, axis=1, keepdims=True)

    pieces = 8
    step = npoints // pieces

    def near_start(cents):
        cent = cents[...]
        csq[...] = jnp.sum(jnp.square(cent.astype(F32)), axis=1, keepdims=True)
        scaled[...] = (cent * (-2.0)).astype(BF16)
        squares[...] = jnp.zeros(squares.shape, F32)

    def near_piece(k, data, i):
        at = pl.ds(pl.multiple_of(i * step, step), step)
        block = data[at, :]
        cross = lax.dot_general(scaled[...], block, (((1,), (1,)), ((), ())),
                                preferred_element_type=F32)
        mins[k, :, at] = jnp.min(cross + csq[...], axis=0, keepdims=True)
        sq = jnp.square(block.astype(F32))
        squares[...] += jnp.sum(sq.reshape(step // 8, 8, width), axis=0)

    def exchange(k, data, cents, table, base, share_out):
        def row(g):
            return table.at[pl.ds(pl.multiple_of(base + g * size, size), size), :]

        def rs(way, j):
            g = j + (parts if way == 1 else 0)
            land = from_left if way == 1 else from_right
            return to("pts", sums.at[part(g), :], land.at[k, j], rs_send.at[k, way, j],
                      rs_recv.at[k, way, j], p + 1 if way == 1 else p - 1)

        def ag(way, j):
            g = j + (parts if way == 1 else 0)
            return to("pts", row(g), row(g), ag_send.at[k, way, j], ag_recv.at[k, way, j],
                      p - 1 if way == 1 else p + 1)

        def block(col, g):
            at = pl.multiple_of(col * rows + g * size, size)
            return codebook.at[pl.ds(at, size), :]

        def x_copy(o, g):
            return to("cb", block(c, g), block(c, g), x_send.at[o, g], x_recv.at[o, g],
                      ((cx + o) % nx) * CORES + cc)

        def d_copy(o, g):
            ref = block(((cx + nx - o) % nx) * CORES + cc, g)
            return to("cb", ref, ref, d_send.at[o, g], d_recv.at[o, g], sibling)

        def spread(g):
            if share_out:
                for o in range(1, nx):
                    x_copy(o, g).start()
                d_copy(0, g).start()

        def run(i, carry):
            for way in (1, 0):
                first, end = (0, last) if way == 1 else (last, 0)
                shift = parts if way == 1 else 0
                near_end = p if way == 1 else last - p
                j = i - lag * near_end

                @pl.when(jnp.logical_and(j >= 0, j < parts))
                def _():
                    @pl.when(p != first)
                    def _():
                        rs(way, j).wait_recv()
                        land = from_left if way == 1 else from_right
                        sums[part(j + shift), :] += land[k, j]

                    @pl.when(p != end)
                    def _():
                        @pl.when(j >= window)
                        def _():
                            rs(way, j - window).wait_send()

                        rs(way, j).start()

                    @pl.when(p == end)
                    def _():
                        g = j + shift
                        old = cents[part(g), :].astype(F32)
                        row(g)[...] = (
                            (sums[part(g), :] + old) / (count(k, g) + 1.0)
                        ).astype(BF16)
                        ag(way, j).start()
                        spread(g)

                back = i - lag * (2 * last) + lag * near_end

                @pl.when(jnp.logical_and(p != end, jnp.logical_and(back >= 0, back < parts)))
                def _():
                    ag(way, back).wait_recv()

                    @pl.when(p != first)
                    def _():
                        ag(way, back).start()

                    spread(back + shift)

                if share_out:
                    over = back - lag

                    @pl.when(jnp.logical_and(over >= 0, over < parts))
                    def _():
                        for o in range(1, nx):
                            x_copy(o, over + shift).wait_recv()
                            d_copy(o, over + shift).start()

            @pl.when(i < pieces)
            def _():
                near_piece(k, data, i)

            if k == 0:
                @pl.when(i == lag)
                def _():
                    for kk in range(2):
                        for d in range(1, npts):
                            code_copy(kk, d, (p + npts - d) % npts).wait()
            else:
                @pl.when(i == pieces)
                def _():
                    for d in range(1, ncb):
                        min_copy(d).start()

                @pl.when(i == pieces + 2 * lag)
                def _():
                    totals()

            return carry

        steps = parts + 2 * lag * last + (lag if share_out else 0)
        lax.fori_loop(0, max(steps, pieces + 2 * lag + 1), run, 0)

        def drain(j, carry):
            for way in (1, 0):
                first, end = (0, last) if way == 1 else (last, 0)
                shift = parts if way == 1 else 0

                @pl.when(jnp.logical_and(p != end, j >= parts - window))
                def _():
                    rs(way, j).wait_send()

                @pl.when(p != first)
                def _():
                    ag(way, j).wait_send()

                if share_out:
                    for o in range(nx):
                        d_copy(o, j + shift).wait()
                        if o > 0:
                            x_copy(o, j + shift).wait_send()
            return carry

        lax.fori_loop(0, parts, drain, 0)

    def min_copy(d):
        return to("cb", mins, mins_in.at[d], min_send.at[d], min_recv.at[d], (c + d) % ncb)

    def tot_copy(d):
        return to("pts", tot, tot_in.at[d], tot_send.at[d], tot_recv.at[d], (p + d) % npts)

    def totals():
        for d in range(1, ncb):
            min_copy(d).wait()
        best = mins[...]
        for d in range(1, ncb):
            best = jnp.minimum(best, mins_in[d])
        squares_two = jnp.sum(squares[...], keepdims=True)
        for k in range(2):
            sq = squares_two if k == 1 else tot[0, :, :1]
            tot[k] = jnp.broadcast_to(jnp.sum(best[k], keepdims=True) + sq, tot.shape[1:])
        for d in range(1, npts):
            tot_copy(d).start()

    partial_sums(points, code_one)
    near_start(cent_one)
    pl.semaphore_wait(barrier, npts - 1 + ncb - 1)
    for k, code in enumerate((code_one, code_two)):
        for d in range(1, npts):
            code_copy(k, d, p).start()
        codes_all[k, p] = code[...]
    exchange(0, points, cent_one, codebook, c * rows, True)
    tot[0] = jnp.broadcast_to(jnp.sum(squares[...], keepdims=True), tot.shape[1:])

    tile = 128
    group = 4

    def look(i, carry):
        blocks = []
        for j in range(group):
            at = pl.ds(pl.multiple_of((i * group + j) * tile, tile), tile)
            blocks.append(jnp.broadcast_to(code_one[:, at], (tile, tile)).T)
        column = jnp.concatenate(blocks, axis=0)
        wide = jnp.concatenate([column] * (ids // tile), axis=1)
        label = lax.broadcasted_iota(jnp.int32, (group * tile, ids), 1)
        onehot = jnp.where(wide == label, 1.0, 0.0).astype(BF16)
        looked = jnp.dot(onehot, codebook[...], preferred_element_type=F32)
        at = pl.ds(pl.multiple_of(i * group * tile, group * tile), group * tile)
        residual[at, :] = (points[at, :].astype(F32) - looked).astype(BF16)
        return carry

    lax.fori_loop(0, npoints // (group * tile), look, 0)
    partial_sums(residual, code_two)
    near_start(cent_two)
    exchange(1, residual, cent_two, new_two, 0, False)
    new_one[...] = codebook[pl.ds(pl.multiple_of(c * rows, rows), rows), :]
    for d in range(1, npts):
        tot_copy(d).wait()
    total = tot[...]
    for d in range(1, npts):
        total = total + tot_in[d]
    total_out[...] = total / F32(npoints * npts * width)


def fused(points, code_one, code_two, cent_one, cent_two):
    npts = lax.axis_size("pts")
    ncb = lax.axis_size("cb")
    npoints, width = points.shape
    rows = cent_one.shape[0]
    nx = ncb // CORES
    parts = PARTS
    size = rows // (2 * parts)
    vmem = pl.BlockSpec(memory_space=pltpu.VMEM)
    dma = pltpu.SemaphoreType.DMA
    new_one, new_two, total = pl.pallas_call(
        functools.partial(fused_kernel, npts, ncb, parts, LAG, WINDOW),
        out_shape=(
            jax.ShapeDtypeStruct(cent_one.shape, BF16),
            jax.ShapeDtypeStruct(cent_two.shape, BF16),
            jax.ShapeDtypeStruct((2, 1, 128), F32),
        ),
        in_specs=[vmem] * 5,
        out_specs=(vmem,) * 3,
        scratch_shapes=[
            pltpu.VMEM(points.shape, BF16),
            pltpu.VMEM((rows * ncb, width), BF16),
            pltpu.VMEM((rows, width), F32),
            pltpu.VMEM((2, parts, size, width), F32),
            pltpu.VMEM((2, parts, size, width), F32),
            pltpu.VMEM((2, npts, 1, npoints), jnp.int32),
            pltpu.VMEM((2, 1, npoints), F32),
            pltpu.VMEM((ncb, 2, 1, npoints), F32),
            pltpu.VMEM((2, 1, 128), F32),
            pltpu.VMEM((npts, 2, 1, 128), F32),
            pltpu.VMEM((rows, width), BF16),
            pltpu.VMEM((rows, 1), F32),
            pltpu.VMEM((8, width), F32),
            dma((2, 2, parts)), dma((2, 2, parts)), dma((2, 2, parts)), dma((2, 2, parts)),
            dma((nx, 2 * parts)), dma((nx, 2 * parts)), dma((nx, 2 * parts)),
            dma((nx, 2 * parts)),
            dma((2, npts)), dma((2, npts)), dma((ncb,)), dma((ncb,)), dma((npts,)), dma((npts,)),
        ],
        compiler_params=pltpu.CompilerParams(
            collective_id=0, has_side_effects=True, vmem_limit_bytes=60 * 1024 * 1024
        ),
    )(points, code_one.reshape(1, npoints), code_two.reshape(1, npoints), cent_one, cent_two)
    return new_one, new_two, total[:, 0, 0]


def nearest_local(data, cents):
    sq = jnp.sum(jnp.square(data.astype(jnp.float32)), axis=1)
    csq = jnp.sum(jnp.square(cents.astype(jnp.float32)), axis=1)
    cross = lax.dot_general(
        data, cents, (((1,), (1,)), ((), ())), preferred_element_type=jnp.float32
    )
    dist = sq[:, None] - 2.0 * cross + csq[None, :]
    local_min = jnp.min(dist, axis=1)
    best = lax.pmin(local_min, "cb")
    return jnp.sum(best)


def section_update(data, codes, cents):
    rows = cents.shape[0]
    first = lax.axis_index("cb") * rows
    labels = first + lax.broadcasted_iota(jnp.int32, (1, rows), 1)
    onehot = (codes[:, None] == labels).astype(jnp.bfloat16)
    sums = lax.dot_general(
        onehot, data, (((0,), (0,)), ((), ())), preferred_element_type=jnp.float32
    )
    counts = jnp.sum(onehot.astype(jnp.float32), axis=0)
    share_sums, share_counts = (
        lax.psum_scatter(sums, "pts", scatter_dimension=0, tiled=True),
        lax.psum_scatter(counts, "pts", scatter_dimension=0, tiled=True),
    )
    share_rows = share_sums.shape[0]
    old_rows = lax.dynamic_slice_in_dim(cents, lax.axis_index("pts") * share_rows, share_rows, 0)
    return ((share_sums + old_rows.astype(jnp.float32)) / (share_counts + 1.0)[:, None]).astype(
        jnp.bfloat16
    )


def section_total(value):
    return lax.psum(value, "pts")


def local(points, code_one, code_two, cent_one, cent_two):
    rows = cent_one.shape[0]
    width = points.shape[1]
    npts = lax.axis_size("pts")
    ncb = lax.axis_size("cb")
    first = lax.axis_index("cb") * rows
    first_local = nearest_local(points, cent_one)
    updated_one = section_update(points, code_one, cent_one)
    gathered = lax.all_gather(updated_one, ("pts", "cb"), axis=0, tiled=True)
    share_rows = updated_one.shape[0]
    codebook = jnp.swapaxes(gathered.reshape(npts, ncb, share_rows, width), 0, 1).reshape(
        rows * ncb, width
    )
    new_one = lax.dynamic_slice_in_dim(codebook, first, rows, 0)
    looked = jnp.take(codebook, code_one, axis=0)
    residual = (points.astype(jnp.float32) - looked.astype(jnp.float32)).astype(jnp.bfloat16)
    updated_two = section_update(residual, code_two, cent_two)
    new_two = lax.all_gather(updated_two, "pts", axis=0, tiled=True)
    second_local = nearest_local(residual, cent_two)
    first_sum = section_total(first_local)
    second_sum = section_total(second_local)
    scale = jnp.float32(points.shape[0] * npts * width)
    distortion = jnp.stack([first_sum, second_sum]) / scale
    return (new_one, new_two, distortion)


def choose(points, code_one, code_two, cent_one, cent_two):
    rows, npts, ncb = cent_one.shape[0], lax.axis_size("pts"), lax.axis_size("cb")
    fits = (
        1 < npts <= 8
        and rows % (32 * PARTS) == 0
        and rows % (16 * npts) == 0
        and ncb % CORES == 0
        and points.shape[0] % 1024 == 0
    )
    form = fused if fits else local
    return form(points, code_one, code_two, cent_one, cent_two)


def solution(mesh):
    return jax.shard_map(
        choose,
        mesh=mesh,
        in_specs=(
            P(("groups", "pts"), None),
            P(("groups", "pts")),
            P(("groups", "pts")),
            P(("groups", "cb"), None),
            P(("groups", "cb"), None),
        ),
        out_specs=(P(("groups", "cb"), None), P(("groups", "cb"), None), P("groups")),
        check_vma=False,
    )
```

profile of v0, /device:TPU:0, one launch (start us, length us, event | category | flops | bytes accessed | tf_op | source)
XLA Modules:
  0.0 111.2 jit_solution(5744142002388637611)
XLA Ops:
  0.6 105.2 %shard_map.76 = (bf16[512,768]{1,0:T(8,128)(2,1)}, bf16[512,768]{1,0:T(8,128)(2,1)}, f32[2,1,128]{2,1,0:T(1,128)}) custom-call(bf16[2048,768]{1,0:T(8,128)(2,1)} %points.1, s32[1,2048]{1,0:T(1,128)} %bitcast.2, s32[1,2048]{1,0:T(1,128)} %bitcast.3, bf16[512,768]{1,0:T(8,128)(2,1)} %cent_one.1, bf16[512,768]{1,0:T(8,128)(2,1)} %cent_two.1), custom_call_target="tpu_custom_call" | custom-call | tf_op jit(solution)/shard_map/pallas_call | solution.py:300
  105.8 1.3 %slice_reduce_fusion = f32[2]{0:T(128)} fusion(f32[2,1,128]{2,1,0:T(1,128)} %get-tuple-element.8), kind=kLoop, calls=%fused_computation | loop fusion | bytes 16 | tf_op jit(solution)/shard_map/slice | solution.py:332
  107.1 2.1 %copy.10 = bf16[512,768]{1,0:T(8,128)(2,1)} copy(bf16[512,768]{1,0:T(8,128)(2,1)} %get-tuple-element.12) | data formatting | bytes 1572864
  109.2 2.1 %copy.11 = bf16[512,768]{1,0:T(8,128)(2,1)} copy(bf16[512,768]{1,0:T(8,128)(2,1)} %get-tuple-element.13) | data formatting | bytes 1572864
where the time goes:
time: 111 us
  Pallas kernels  105 us (95%)
  local copies, waits for them, and re-layouts  5.4 us (5%)
    pallas_call x1, Pallas kernels, fused(): pl.pallas_call(functools.partial(fused_kernel, npts, ncb, parts, LAG, WIN...  105 us
    unnamed x2, local copies, waits for them, and re-layouts  4.12 us

commit v1 on v0

v1 whole, which is shorter than its diff:
```python
import functools

import jax
import jax.numpy as jnp
from jax import lax
from jax.experimental import pallas as pl
from jax.experimental.pallas import tpu as pltpu
from jax.sharding import PartitionSpec as P

F32 = jnp.float32
BF16 = jnp.bfloat16
I16 = jnp.int16
CORES = 2
SIZE = 32
SPAN = 128
GROUP = 64
PIECES = 8
HOP = 3
TOP = 32700.0
TINY = 2.0 ** -100
LOWEST = -16
BITS = 7


def fused_kernel(
    npts, ncb,
    points, code_one, code_two, cent_one, cent_two,
    new_one, new_two, total_out,
    residual, codebook, sums, quant, quant_in, meta, meta_in, cols, ones, column,
    mins, mins_in, tot, tot_in, scaled, csq, squares,
    up_send, up_recv, swap_send, swap_recv, down_send, down_recv,
    mup_send, mup_recv, mswap_send, mswap_recv,
    x_send, x_recv, d_send, d_recv, min_send, min_recv, tot_send, tot_recv,
):
    p = lax.axis_index("pts")
    c = lax.axis_index("cb")
    npoints, width = points.shape
    rows = cent_one.shape[0]
    n = rows // SIZE
    per = SPAN // SIZE
    nx = ncb // CORES
    cx, cc = c // CORES, c % CORES
    sibling = cx * CORES + (1 - cc)
    side = p // 2
    inner = jnp.logical_or(p == 1, p == 2)
    outer = jnp.logical_not(inner)
    pair = p + 1 - 2 * (p % 2)
    across = npts - 1 - p

    def to(axis, src, dst, s, r, where):
        return pltpu.make_async_remote_copy(
            src_ref=src, dst_ref=dst, send_sem=s, recv_sem=r,
            device_id={axis: where}, device_id_type=pl.DeviceIdType.MESH,
        )

    barrier = pltpu.get_barrier_semaphore()
    for d in range(1, npts):
        pl.semaphore_signal(barrier, inc=1, device_id={"pts": (p + d) % npts},
                            device_id_type=pl.DeviceIdType.MESH)
    for d in range(1, ncb):
        pl.semaphore_signal(barrier, inc=1, device_id={"cb": (c + d) % ncb},
                            device_id_type=pl.DeviceIdType.MESH)

    def span(start, length):
        return pl.ds(pl.multiple_of(start, length), length)

    def chunk(j):
        return span(j * SIZE, SIZE)

    def up(k, j):
        return to("pts", quant.at[k, side, chunk(j), :], quant_in.at[k, chunk(j), :],
                  up_send.at[k, j], up_recv.at[k, j], pair)

    def swap(k, j):
        ref = quant.at[k, side, chunk(j), :]
        return to("pts", ref, ref, swap_send.at[k, j], swap_recv.at[k, j], across)

    def meta_up(k, t):
        return to("pts", meta.at[k, side, t], meta_in.at[k, t], mup_send.at[k, t],
                  mup_recv.at[k, t], pair)

    def meta_swap(k, t):
        ref = meta.at[k, side, t]
        return to("pts", ref, ref, mswap_send.at[k, t], mswap_recv.at[k, t], across)

    def block(col, j):
        first = j * SIZE
        at = (first // GROUP) * (GROUP * ncb) + col * GROUP + first % GROUP
        return codebook.at[span(at, SIZE), :]

    def fresh(k, j):
        return block(c, j) if k == 0 else new_two.at[chunk(j), :]

    def down(k, j):
        return to("pts", fresh(k, j), fresh(k, j), down_send.at[k, j], down_recv.at[k, j], pair)

    def x_copy(o, j):
        return to("cb", block(c, j), block(c, j), x_send.at[o, j], x_recv.at[o, j],
                  ((cx + o) % nx) * CORES + cc)

    def d_copy(o, j):
        ref = block(((cx + nx - o) % nx) * CORES + cc, j)
        return to("cb", ref, ref, d_send.at[o, j], d_recv.at[o, j], sibling)

    def spread(k, j):
        if k == 0:
            for o in range(1, nx):
                x_copy(o, j).start()
            d_copy(0, j).start()

    def min_copy(d):
        return to("cb", mins, mins_in.at[d], min_send.at[d], min_recv.at[d], (c + d) % ncb)

    def tot_copy(d):
        return to("pts", tot, tot_in.at[p], tot_send.at[d], tot_recv.at[d], (p + d) % npts)

    def eye():
        return (lax.broadcasted_iota(jnp.int32, (SPAN, SPAN), 0)
                == lax.broadcasted_iota(jnp.int32, (SPAN, SPAN), 1))

    def lanes(col):
        return jnp.sum(jnp.where(eye(), col, 0.0), axis=0, keepdims=True)

    def upright(row):
        return jnp.sum(jnp.where(eye(), row, 0.0), axis=1, keepdims=True)

    def scale_of(high):
        power = jnp.floor(jnp.log2(TOP / jnp.maximum(high, TINY))).astype(jnp.int32)
        power = jnp.clip(power - LOWEST, 0, 2 ** BITS - 1)
        ratio = jnp.full(high.shape, 2.0 ** LOWEST, F32)
        unit = jnp.full(high.shape, 2.0 ** -LOWEST, F32)
        for bit in range(BITS):
            on = (power // 2 ** bit) % 2 == 1
            ratio = ratio * jnp.where(on, 2.0 ** (2 ** bit), 1.0)
            unit = unit * jnp.where(on, 2.0 ** -(2 ** bit), 1.0)
        return ratio, unit

    def code16(values, ratio):
        return jnp.round(values * ratio).astype(jnp.int32).astype(I16)

    def wide(codes, unit):
        return codes.astype(jnp.int32).astype(F32) * unit

    def pieces_of_sums(k, data, code):
        def one(t, carry):
            with jax.named_scope("sums"):
                label = c * rows + t * SPAN + lax.broadcasted_iota(jnp.int32, (SPAN, npoints), 0)
                hot = jnp.where(code[...] == label, 1.0, 0.0)
                at = span(t * SPAN, SPAN)
                part = jnp.dot(hot.astype(BF16), data[...], preferred_element_type=F32)
                sums[at, :] = part
                ones[0, t] = lanes(jnp.max(jnp.abs(part), axis=1, keepdims=True))
                ones[1, t] = lanes(jnp.sum(hot, axis=1, keepdims=True))

            if k == 0:
                @pl.when(t == 0)
                def _():
                    with jax.named_scope("barrier"):
                        pl.semaphore_wait(barrier, npts - 1 + ncb - 1)

            @pl.when(outer)
            def _():
                with jax.named_scope("quant"):
                    ratio, unit = scale_of(ones[0, t])
                    meta[k, side, t, 0:1, :] = ones[0, t]
                    meta[k, side, t, 1:2, :] = ones[1, t]
                    meta[k, side, t, 2:3, :] = unit
                    meta_up(k, t).start()
                    quant[k, side, at, :] = code16(sums[at, :], upright(ratio))
                    for jj in range(per):
                        up(k, t * per + jj).start()

            return carry

        lax.fori_loop(0, rows // SPAN, one, 0)

    @jax.named_scope("join")
    def join(k, j):
        t = j // per

        @pl.when(j % per == 0)
        def _():
            meta_up(k, t).wait_recv()
            at = span(t * SPAN, SPAN)
            ratio, unit = scale_of(meta_in[k, t, 0:1, :] + ones[0, t])
            meta[k, side, t, 1:2, :] = meta_in[k, t, 1:2, :] + ones[1, t]
            meta[k, side, t, 2:3, :] = unit
            meta_swap(k, t).start()
            cols[0, at, :] = upright(meta_in[k, t, 2:3, :])
            cols[1, at, :] = upright(ratio)

        with jax.named_scope("join_wait"):
            up(k, j).wait_recv()
        at = chunk(j)
        both = sums[at, :] + wide(quant_in[k, at, :], cols[0, at, :])
        quant[k, side, at, :] = code16(both, cols[1, at, :])
        swap(k, j).start()

    @jax.named_scope("settle")
    def settle(k, j, cents):
        t = j // per

        @pl.when(j % per == 0)
        def _():
            meta_swap(k, t).wait_recv()
            at = span(t * SPAN, SPAN)
            share = 1.0 / (meta[k, 0, t, 1:2, :] + meta[k, 1, t, 1:2, :] + 1.0)
            cols[2, at, :] = upright(meta[k, 0, t, 2:3, :])
            cols[3, at, :] = upright(meta[k, 1, t, 2:3, :])
            cols[4, at, :] = upright(share)

        with jax.named_scope("settle_wait"):
            swap(k, j).wait_recv()
        at = chunk(j)
        low = wide(quant[k, 0, at, :], cols[2, at, :])
        high = wide(quant[k, 1, at, :], cols[3, at, :])
        old = cents[at, :].astype(F32)
        fresh(k, j)[...] = ((low + high + old) * cols[4, at, :]).astype(BF16)
        down(k, j).start()
        spread(k, j)

    step = npoints // PIECES

    @jax.named_scope("near_start")
    def near_start(cents):
        cent = cents[...]
        csq[...] = jnp.sum(jnp.square(cent.astype(F32)), axis=1, keepdims=True)
        scaled[...] = (cent * (-2.0)).astype(BF16)
        squares[...] = jnp.zeros(squares.shape, F32)

    @jax.named_scope("near")
    def near_piece(k, data, i):
        at = span(i * step, step)
        rows_in = data[at, :]
        cross = lax.dot_general(scaled[...], rows_in, (((1,), (1,)), ((), ())),
                                preferred_element_type=F32)
        mins[k, :, at] = jnp.min(cross + csq[...], axis=0, keepdims=True)
        sq = jnp.square(rows_in.astype(F32))
        squares[...] += jnp.sum(sq.reshape(step // 8, 8, width), axis=0)

    tile = 128
    setups = 4

    @jax.named_scope("setup")
    def setup(i):
        for j in range(npoints // (tile * setups)):
            at = span(i * (npoints // setups) + j * tile, tile)
            column[at, :] = jnp.broadcast_to(code_one[:, at], (tile, tile)).T
        at = span(i * (npoints // setups), npoints // setups)
        residual[at, :] = points[at, :]

    halves = GROUP // SIZE
    depth = GROUP * ncb
    look_step = 1024

    @jax.named_scope("look")
    def look(b, h):
        @pl.when(h == 0)
        def _():
            for jj in range(halves):
                for o in range(nx):
                    with jax.named_scope("d_wait"):
                        d_copy(o, b * halves + jj).wait_recv()

        labels = []
        for q in range(depth // tile):
            lane = q * tile + lax.broadcasted_iota(jnp.int32, (look_step, tile), 1)
            labels.append((lane // GROUP) * rows + lane % GROUP + b * GROUP)

        def one(s, carry):
            at = span(h * (npoints // halves) + s * look_step, look_step)
            held = column[at, :]
            hot = jnp.concatenate(
                [jnp.where(held == label, 1.0, 0.0).astype(BF16) for label in labels], axis=1
            )
            found = jnp.dot(hot, codebook[span(b * depth, depth), :], preferred_element_type=F32)
            residual[at, :] = (residual[at, :].astype(F32) - found).astype(BF16)
            return carry

        lax.fori_loop(0, npoints // (halves * look_step), one, 0)

    @jax.named_scope("totals")
    def totals():
        for d in range(1, ncb):
            min_copy(d).wait()
        best = mins[...]
        for d in range(1, ncb):
            best = jnp.minimum(best, mins_in[d])
        squares_two = jnp.sum(squares[...], keepdims=True)
        for k in range(2):
            sq = squares_two if k == 1 else tot[0, :, :1]
            tot[k] = jnp.broadcast_to(jnp.sum(best[k], keepdims=True) + sq, tot.shape[1:])
        for d in range(1, npts):
            tot_copy(d).start()

    def exchange(k, data, cents):
        lag_join = HOP
        lag_settle = 2 * HOP
        lag_down = 3 * HOP
        lag_x = jnp.where(inner, 3 * HOP, 4 * HOP)

        def run(i, carry):
            @pl.when(inner)
            def _():
                j = i - lag_settle

                @pl.when(jnp.logical_and(j >= 0, j < n))
                def _():
                    settle(k, j, cents)

                j = i - lag_join

                @pl.when(jnp.logical_and(j >= 0, j < n))
                def _():
                    join(k, j)

            @pl.when(outer)
            def _():
                j = i - lag_down

                @pl.when(jnp.logical_and(j >= 0, j < n))
                def _():
                    with jax.named_scope("down_wait"):
                        down(k, j).wait_recv()
                    spread(k, j)

            @pl.when(i < PIECES)
            def _():
                near_piece(k, data, i)

            if k == 0:
                @pl.when(jnp.logical_and(i >= PIECES, i < PIECES + setups))
                def _():
                    setup(i - PIECES)

                j = i - lag_x

                @pl.when(jnp.logical_and(j >= 0, j < n))
                def _():
                    for o in range(1, nx):
                        with jax.named_scope("x_wait"):
                            x_copy(o, j).wait_recv()
                        d_copy(o, j).start()

                v = i - lag_x - halves - 1

                @pl.when(jnp.logical_and(v >= 0, v < n))
                def _():
                    look(v // halves, v % halves)
            else:
                @pl.when(i == PIECES)
                def _():
                    for d in range(1, ncb):
                        min_copy(d).start()

                @pl.when(i == PIECES + 2 * HOP)
                def _():
                    totals()

            return carry

        steps = n + 4 * HOP + halves + 1 if k == 0 else n + 3 * HOP
        lax.fori_loop(0, steps, run, 0)

    pieces_of_sums(0, points, code_one)
    near_start(cent_one)
    exchange(0, points, cent_one)
    tot[0] = jnp.broadcast_to(jnp.sum(squares[...], keepdims=True), tot.shape[1:])
    pieces_of_sums(1, residual, code_two)
    near_start(cent_two)
    for g in range(rows // GROUP):
        new_one[g * GROUP:(g + 1) * GROUP, :] = codebook[span(g * depth + c * GROUP, GROUP), :]
    exchange(1, residual, cent_two)

    def drain(j, carry):
        for k in range(2):
            @pl.when(outer)
            def _():
                up(k, j).wait_send()

            @pl.when(inner)
            def _():
                swap(k, j).wait_send()
                down(k, j).wait_send()
        for o in range(nx):
            d_copy(o, j).wait_send()
            if o > 0:
                x_copy(o, j).wait_send()
        return carry

    lax.fori_loop(0, n, drain, 0)
    for k in range(2):
        for t in range(rows // SPAN):
            @pl.when(outer)
            def _():
                meta_up(k, t).wait_send()

            @pl.when(inner)
            def _():
                meta_swap(k, t).wait_send()
    for d in range(1, npts):
        tot_copy(d).wait()
    tot_in[p] = tot[...]
    total = tot_in[0]
    for d in range(1, npts):
        total = total + tot_in[d]
    total_out[...] = total / F32(npoints * npts * width)


def fused(points, code_one, code_two, cent_one, cent_two):
    npts = lax.axis_size("pts")
    ncb = lax.axis_size("cb")
    npoints, width = points.shape
    rows = cent_one.shape[0]
    nx = ncb // CORES
    n = rows // SIZE
    spans = rows // SPAN
    vmem = pl.BlockSpec(memory_space=pltpu.VMEM)
    dma = pltpu.SemaphoreType.DMA
    new_one, new_two, total = pl.pallas_call(
        functools.partial(fused_kernel, npts, ncb),
        out_shape=(
            jax.ShapeDtypeStruct(cent_one.shape, BF16),
            jax.ShapeDtypeStruct(cent_two.shape, BF16),
            jax.ShapeDtypeStruct((2, 1, 128), F32),
        ),
        in_specs=[vmem] * 5,
        out_specs=(vmem,) * 3,
        scratch_shapes=[
            pltpu.VMEM(points.shape, BF16),
            pltpu.VMEM((rows * ncb, width), BF16),
            pltpu.VMEM((rows, width), F32),
            pltpu.VMEM((2, 2, rows, width), I16),
            pltpu.VMEM((2, rows, width), I16),
            pltpu.VMEM((2, 2, spans, 4, SPAN), F32),
            pltpu.VMEM((2, spans, 4, SPAN), F32),
            pltpu.VMEM((5, rows, 1), F32),
            pltpu.VMEM((2, spans, 1, SPAN), F32),
            pltpu.VMEM((npoints, 128), jnp.int32),
            pltpu.VMEM((2, 1, npoints), F32),
            pltpu.VMEM((ncb, 2, 1, npoints), F32),
            pltpu.VMEM((2, 1, 128), F32),
            pltpu.VMEM((npts, 2, 1, 128), F32),
            pltpu.VMEM((rows, width), BF16),
            pltpu.VMEM((rows, 1), F32),
            pltpu.VMEM((8, width), F32),
            dma((2, n)), dma((2, n)), dma((2, n)), dma((2, n)), dma((2, n)), dma((2, n)),
            dma((2, spans)), dma((2, spans)), dma((2, spans)), dma((2, spans)),
            dma((nx, n)), dma((nx, n)), dma((nx, n)), dma((nx, n)),
            dma((ncb,)), dma((ncb,)), dma((npts,)), dma((npts,)),
        ],
        compiler_params=pltpu.CompilerParams(
            collective_id=0, has_side_effects=True, vmem_limit_bytes=60 * 1024 * 1024
        ),
    )(points, code_one.reshape(1, npoints), code_two.reshape(1, npoints), cent_one, cent_two)
    return new_one, new_two, total[:, 0, 0]


def nearest_local(data, cents):
    sq = jnp.sum(jnp.square(data.astype(jnp.float32)), axis=1)
    csq = jnp.sum(jnp.square(cents.astype(jnp.float32)), axis=1)
    cross = lax.dot_general(
        data, cents, (((1,), (1,)), ((), ())), preferred_element_type=jnp.float32
    )
    dist = sq[:, None] - 2.0 * cross + csq[None, :]
    local_min = jnp.min(dist, axis=1)
    best = lax.pmin(local_min, "cb")
    return jnp.sum(best)


def section_update(data, codes, cents):
    rows = cents.shape[0]
    first = lax.axis_index("cb") * rows
    labels = first + lax.broadcasted_iota(jnp.int32, (1, rows), 1)
    onehot = (codes[:, None] == labels).astype(jnp.bfloat16)
    sums = lax.dot_general(
        onehot, data, (((0,), (0,)), ((), ())), preferred_element_type=jnp.float32
    )
    counts = jnp.sum(onehot.astype(jnp.float32), axis=0)
    share_sums, share_counts = (
        lax.psum_scatter(sums, "pts", scatter_dimension=0, tiled=True),
        lax.psum_scatter(counts, "pts", scatter_dimension=0, tiled=True),
    )
    share_rows = share_sums.shape[0]
    old_rows = lax.dynamic_slice_in_dim(cents, lax.axis_index("pts") * share_rows, share_rows, 0)
    return ((share_sums + old_rows.astype(jnp.float32)) / (share_counts + 1.0)[:, None]).astype(
        jnp.bfloat16
    )


def section_total(value):
    return lax.psum(value, "pts")


def local(points, code_one, code_two, cent_one, cent_two):
    rows = cent_one.shape[0]
    width = points.shape[1]
    npts = lax.axis_size("pts")
    ncb = lax.axis_size("cb")
    first = lax.axis_index("cb") * rows
    first_local = nearest_local(points, cent_one)
    updated_one = section_update(points, code_one, cent_one)
    gathered = lax.all_gather(updated_one, ("pts", "cb"), axis=0, tiled=True)
    share_rows = updated_one.shape[0]
    codebook = jnp.swapaxes(gathered.reshape(npts, ncb, share_rows, width), 0, 1).reshape(
        rows * ncb, width
    )
    new_one = lax.dynamic_slice_in_dim(codebook, first, rows, 0)
    looked = jnp.take(codebook, code_one, axis=0)
    residual = (points.astype(jnp.float32) - looked.astype(jnp.float32)).astype(jnp.bfloat16)
    updated_two = section_update(residual, code_two, cent_two)
    new_two = lax.all_gather(updated_two, "pts", axis=0, tiled=True)
    second_local = nearest_local(residual, cent_two)
    first_sum = section_total(first_local)
    second_sum = section_total(second_local)
    scale = jnp.float32(points.shape[0] * npts * width)
    distortion = jnp.stack([first_sum, second_sum]) / scale
    return (new_one, new_two, distortion)


def choose(points, code_one, code_two, cent_one, cent_two):
    rows, npts, ncb = cent_one.shape[0], lax.axis_size("pts"), lax.axis_size("cb")
    fits = (
        npts == 4
        and ncb % CORES == 0
        and (ncb * GROUP) % 128 == 0
        and rows % SPAN == 0
        and points.shape[0] % 2048 == 0
    )
    form = fused if fits else local
    return form(points, code_one, code_two, cent_one, cent_two)


def solution(mesh):
    return jax.shard_map(
        choose,
        mesh=mesh,
        in_specs=(
            P(("groups", "pts"), None),
            P(("groups", "pts")),
            P(("groups", "pts")),
            P(("groups", "cb"), None),
            P(("groups", "cb"), None),
        ),
        out_specs=(P(("groups", "cb"), None), P(("groups", "cb"), None), P("groups")),
        check_vma=False,
    )
```

time: 111 us -> 81.6 us (0.74)
  Pallas kernels: 105 us -> 75.3 us
    pallas_call x1, Pallas kernels: 105 us -> 75.3 us  [fused(): pl.pallas_call(functools.partial(fused_kernel, npts, ncb), out_shape=(jax...]
where the time goes in v1:
time: 81.6 us; the launch traced here: 81.4 us
  Pallas kernels  75.3 us (92%)
  local copies, waits for them, and re-layouts  5.4 us (7%)
    pallas_call x1, Pallas kernels, fused(): pl.pallas_call(functools.partial(fused_kernel, npts, ncb), out_shape=(jax...  75.3 us
    unnamed x2, local copies, waits for them, and re-layouts  4.12 us

profile of v1, /device:TPU:0, one launch (start us, length us, event | category | flops | bytes accessed | tf_op | source)
XLA Modules:
  0.0 81.4 jit_solution(17645653738763830111)
XLA Ops:
  0.6 75.3 %shard_map.76 = (bf16[512,768]{1,0:T(8,128)(2,1)}, bf16[512,768]{1,0:T(8,128)(2,1)}, f32[2,1,128]{2,1,0:T(1,128)}) custom-call(bf16[2048,768]{1,0:T(8,128)(2,1)} %points.1, s32[1,2048]{1,0:T(1,128)} %bitcast.2, s32[1,2048]{1,0:T(1,128)} %bitcast.3, bf16[512,768]{1,0:T(8,128)(2,1)} %cent_one.1, bf16[512,768]{1,0:T(8,128)(2,1)} %cent_two.1), custom_call_target="tpu_custom_call" | custom-call | tf_op jit(solution)/shard_map/pallas_call | solution.py:420
  76.0 1.3 %slice_reduce_fusion = f32[2]{0:T(128)} fusion(f32[2,1,128]{2,1,0:T(1,128)} %get-tuple-element.8), kind=kLoop, calls=%fused_computation | loop fusion | bytes 16 | tf_op jit(solution)/shard_map/slice | solution.py:456
  77.3 2.1 %copy.10 = bf16[512,768]{1,0:T(8,128)(2,1)} copy(bf16[512,768]{1,0:T(8,128)(2,1)} %get-tuple-element.12) | data formatting | bytes 1572864
  79.3 2.1 %copy.11 = bf16[512,768]{1,0:T(8,128)(2,1)} copy(bf16[512,768]{1,0:T(8,128)(2,1)} %get-tuple-element.13) | data formatting | bytes 1572864

commit v2 on v1

--- a/solution.py
+++ b/solution.py
@@ -15,7 +15,11 @@
 SPAN = 128
 GROUP = 64
 PIECES = 8
-HOP = 3
+LJ = 3
+LS = 7
+LD = 11
+LX = 4
+LK = 3
 TOP = 32700.0
 TINY = 2.0 ** -100
 LOWEST = -16
@@ -24,14 +28,24 @@
 
 def fused_kernel(
     npts, ncb,
-    points, code_one, code_two, cent_one, cent_two,
+    points_in, code_one_in, code_two_in, cent_one_in, cent_two_in,
     new_one, new_two, total_out,
+    points, code_one, code_two, cent_one, cent_two, load_sem,
     residual, codebook, sums, quant, quant_in, meta, meta_in, cols, ones, column,
     mins, mins_in, tot, tot_in, scaled, csq, squares,
     up_send, up_recv, swap_send, swap_recv, down_send, down_recv,
     mup_send, mup_recv, mswap_send, mswap_recv,
     x_send, x_recv, d_send, d_recv, min_send, min_recv, tot_send, tot_recv,
 ):
+    loads = [
+        pltpu.make_async_copy(src, dst, load_sem.at[at])
+        for at, (src, dst) in enumerate((
+            (code_one_in, code_one), (points_in, points), (cent_one_in, cent_one),
+            (code_two_in, code_two), (cent_two_in, cent_two),
+        ))
+    ]
+    for load in loads:
+        load.start()
     p = lax.axis_index("pts")
     c = lax.axis_index("cb")
     npoints, width = points.shape
@@ -250,6 +264,7 @@
         residual[at, :] = points[at, :]
 
     halves = GROUP // SIZE
+    looks = 2
     depth = GROUP * ncb
     look_step = 1024
 
@@ -268,7 +283,7 @@
             labels.append((lane // GROUP) * rows + lane % GROUP + b * GROUP)
 
         def one(s, carry):
-            at = span(h * (npoints // halves) + s * look_step, look_step)
+            at = span(h * (npoints // looks) + s * look_step, look_step)
             held = column[at, :]
             hot = jnp.concatenate(
                 [jnp.where(held == label, 1.0, 0.0).astype(BF16) for label in labels], axis=1
@@ -277,7 +292,7 @@
             residual[at, :] = (residual[at, :].astype(F32) - found).astype(BF16)
             return carry
 
-        lax.fori_loop(0, npoints // (halves * look_step), one, 0)
+        lax.fori_loop(0, npoints // (looks * look_step), one, 0)
 
     @jax.named_scope("totals")
     def totals():
@@ -294,10 +309,10 @@
             tot_copy(d).start()
 
     def exchange(k, data, cents):
-        lag_join = HOP
-        lag_settle = 2 * HOP
-        lag_down = 3 * HOP
-        lag_x = jnp.where(inner, 3 * HOP, 4 * HOP)
+        lag_join = LJ
+        lag_settle = LS
+        lag_down = LD
+        lag_x = jnp.where(inner, LS, LD) + LX
 
         def run(i, carry):
             @pl.when(inner)
@@ -342,27 +357,34 @@
                             x_copy(o, j).wait_recv()
                         d_copy(o, j).start()
 
-                v = i - lag_x - halves - 1
-
-                @pl.when(jnp.logical_and(v >= 0, v < n))
-                def _():
-                    look(v // halves, v % halves)
+                v = i - lag_x - LK
+
+                every = halves // looks
+
+                @pl.when(jnp.logical_and(v >= 0, jnp.logical_and(v < n, v % every == 0)))
+                def _():
+                    look(v // halves, (v % halves) // every)
             else:
                 @pl.when(i == PIECES)
                 def _():
                     for d in range(1, ncb):
                         min_copy(d).start()
 
-                @pl.when(i == PIECES + 2 * HOP)
+                @pl.when(i == PIECES + 6)
                 def _():
                     totals()
 
             return carry
 
-        steps = n + 4 * HOP + halves + 1 if k == 0 else n + 3 * HOP
+        steps = n + LD + LX + LK if k == 0 else n + LD
         lax.fori_loop(0, steps, run, 0)
 
+    loads[0].wait()
+    loads[1].wait()
     pieces_of_sums(0, points, code_one)
+    loads[2].wait()
+    loads[3].wait()
+    loads[4].wait()
     near_start(cent_one)
     exchange(0, points, cent_one)
     tot[0] = jnp.broadcast_to(jnp.sum(squares[...], keepdims=True), tot.shape[1:])
@@ -405,6 +427,34 @@
     for d in range(1, npts):
         total = total + tot_in[d]
     total_out[...] = total / F32(npoints * npts * width)
+
+
+def finish_kernel(one_in, two_in, total_in, one_out, two_out, total_out, sem):
+    first = pltpu.make_async_copy(one_in, one_out, sem.at[0])
+    second = pltpu.make_async_copy(two_in, two_out, sem.at[1])
+    first.start()
+    second.start()
+    for k in range(2):
+        total_out[k] = jnp.sum(total_in[k, :, :1])
+    first.wait()
+    second.wait()
+
+
+def finish(new_one, new_two, total):
+    vmem = pl.BlockSpec(memory_space=pltpu.VMEM)
+    anywhere = pl.BlockSpec(memory_space=pl.ANY)
+    return pl.pallas_call(
+        finish_kernel,
+        out_shape=(
+            jax.ShapeDtypeStruct(new_one.shape, BF16),
+            jax.ShapeDtypeStruct(new_two.shape, BF16),
+            jax.ShapeDtypeStruct((2,), F32),
+        ),
+        in_specs=[vmem] * 3,
+        out_specs=(anywhere, anywhere, pl.BlockSpec(memory_space=pltpu.SMEM)),
+        scratch_shapes=[pltpu.SemaphoreType.DMA((2,))],
+        compiler_params=pltpu.CompilerParams(vmem_limit_bytes=8 * 1024 * 1024),
+    )(new_one, new_two, total)
 
 
 def fused(points, code_one, code_two, cent_one, cent_two):
@@ -420,13 +470,19 @@
     new_one, new_two, total = pl.pallas_call(
         functools.partial(fused_kernel, npts, ncb),
         out_shape=(
-            jax.ShapeDtypeStruct(cent_one.shape, BF16),
-            jax.ShapeDtypeStruct(cent_two.shape, BF16),
-            jax.ShapeDtypeStruct((2, 1, 128), F32),
+            pltpu.VMEM(cent_one.shape, BF16),
+            pltpu.VMEM(cent_two.shape, BF16),
+            pltpu.VMEM((2, 1, 128), F32),
         ),
-        in_specs=[vmem] * 5,
+        in_specs=[pl.BlockSpec(memory_space=pl.ANY)] * 5,
         out_specs=(vmem,) * 3,
         scratch_shapes=[
+            pltpu.VMEM(points.shape, BF16),
+            pltpu.VMEM((1, npoints), jnp.int32),
+            pltpu.VMEM((1, npoints), jnp.int32),
+            pltpu.VMEM(cent_one.shape, BF16),
+            pltpu.VMEM(cent_two.shape, BF16),
+            dma((5,)),
             pltpu.VMEM(points.shape, BF16),
             pltpu.VMEM((rows * ncb, width), BF16),
             pltpu.VMEM((rows, width), F32),
@@ -453,7 +509,7 @@
             collective_id=0, has_side_effects=True, vmem_limit_bytes=60 * 1024 * 1024
         ),
     )(points, code_one.reshape(1, npoints), code_two.reshape(1, npoints), cent_one, cent_two)
-    return new_one, new_two, total[:, 0, 0]
+    return finish(new_one, new_two, total)
 
 
 def nearest_local(data, cents):

time: 81.6 us -> 71.6 us (0.88)
  local copies, waits for them, and re-layouts: 5.4 us -> 0 us
  Pallas kernels: 75.3 us -> 70.7 us
    pallas_call x1 -> x2, Pallas kernels: 75.3 us -> 70.7 us  [the longest x1 69 us: fused(): pl.pallas_call(functools.partial(fused_kernel, npts, ncb), out_shape=(plt...]
    unnamed x2 -> x0, local copies, waits for them, and re-layouts: 4.12 us -> none
    slice x1 -> x0, local copies, waits for them, and re-layouts: 1.27 us -> none  [fused(): return (new_one, new_two, total[:, 0, 0])]
where the time goes in v2:
time: 71.6 us; the launch traced here: 71.3 us
  Pallas kernels  70.7 us (99%)
    pallas_call x1, Pallas kernels, fused(): pl.pallas_call(functools.partial(fused_kernel, npts, ncb), out_shape=(plt...  69 us
    pallas_call x1, Pallas kernels, finish(): pl.pallas_call(finish_kernel, out_shape=(jax.ShapeDtypeStruct(new_one.sha...  1.67 us

profile of v2, /device:TPU:0, one launch (start us, length us, event | category | flops | bytes accessed | tf_op | source)
XLA Modules:
  0.0 71.3 jit_solution(11849732896436615938)
XLA Ops:
  0.6 69.0 %shard_map.76 = (bf16[512,768]{1,0:T(8,128)(2,1)S(1)}, bf16[512,768]{1,0:T(8,128)(2,1)S(1)}, f32[2,1,128]{2,1,0:T(1,128)S(1)}) custom-call(bf16[2048,768]{1,0:T(8,128)(2,1)} %points_in.1, s32[1,2048]{1,0:T(1,128)} %bitcast.2, s32[1,2048]{1,0:T(1,128)} %bitcast.3, bf16[512,768]{1,0:T(8,128)(2,1)} %cent_one_in.1, bf16[512,768]{1,0:T(8,128)(2,1)} %cent_two_in.1), custom_call_target="tpu_custom_call" | custom-call | tf_op jit(solution)/shard_map/pallas_call | solution.py:470
  69.7 1.7 %shard_map.77 = (bf16[512,768]{1,0:T(8,128)(2,1)}, bf16[512,768]{1,0:T(8,128)(2,1)}, f32[2]{0:T(128)}) custom-call(bf16[512,768]{1,0:T(8,128)(2,1)S(1)} %get-tuple-element.6.one_in, bf16[512,768]{1,0:T(8,128)(2,1)S(1)} %get-tuple-element.7.two_in, f32[2,1,128]{2,1,0:T(1,128)S(1)} %get-tuple-element.8.total_in), custom_call_target="tpu_custom_call" | custom-call | tf_op jit(solution)/shard_map/pallas_call | solution.py:446

commit v3 on v2

--- a/solution.py
+++ b/solution.py
@@ -308,6 +308,31 @@
         for d in range(1, npts):
             tot_copy(d).start()
 
+    def close_first(j):
+        @pl.when(outer)
+        def _():
+            up(0, j).wait_send()
+
+        @pl.when(inner)
+        def _():
+            swap(0, j).wait_send()
+            down(0, j).wait_send()
+
+        for o in range(nx):
+            d_copy(o, j).wait_send()
+            if o > 0:
+                x_copy(o, j).wait_send()
+
+    def close_meta(k):
+        for t in range(rows // SPAN):
+            @pl.when(outer)
+            def _():
+                meta_up(k, t).wait_send()
+
+            @pl.when(inner)
+            def _():
+                meta_swap(k, t).wait_send()
+
     def exchange(k, data, cents):
         lag_join = LJ
         lag_settle = LS
@@ -338,6 +363,8 @@
                     with jax.named_scope("down_wait"):
                         down(k, j).wait_recv()
                     spread(k, j)
+                    if k == 1:
+                        up(1, j).wait_send()
 
             @pl.when(i < PIECES)
             def _():
@@ -365,6 +392,14 @@
                 def _():
                     look(v // halves, (v % halves) // every)
             else:
+                @pl.when(i < n)
+                def _():
+                    close_first(i)
+
+                @pl.when(i == n)
+                def _():
+                    close_meta(0)
+
                 @pl.when(i == PIECES)
                 def _():
                     for d in range(1, ncb):
@@ -394,32 +429,16 @@
         new_one[g * GROUP:(g + 1) * GROUP, :] = codebook[span(g * depth + c * GROUP, GROUP), :]
     exchange(1, residual, cent_two)
 
-    def drain(j, carry):
-        for k in range(2):
-            @pl.when(outer)
-            def _():
-                up(k, j).wait_send()
-
-            @pl.when(inner)
-            def _():
-                swap(k, j).wait_send()
-                down(k, j).wait_send()
-        for o in range(nx):
-            d_copy(o, j).wait_send()
-            if o > 0:
-                x_copy(o, j).wait_send()
-        return carry
-
-    lax.fori_loop(0, n, drain, 0)
-    for k in range(2):
-        for t in range(rows // SPAN):
-            @pl.when(outer)
-            def _():
-                meta_up(k, t).wait_send()
-
-            @pl.when(inner)
-            def _():
-                meta_swap(k, t).wait_send()
+    @pl.when(inner)
+    def _():
+        def drain(j, carry):
+            swap(1, j).wait_send()
+            down(1, j).wait_send()
+            return carry
+
+        lax.fori_loop(0, n, drain, 0)
+
+    close_meta(1)
     for d in range(1, npts):
         tot_copy(d).wait()
     tot_in[p] = tot[...]

time: 71.6 us -> 71.3 us (level)
  no operation moved by 1% of the time
where the time goes in v3:
time: 71.3 us; the launch traced here: 71.1 us
  Pallas kernels  70.5 us (99%)
    pallas_call x1, Pallas kernels, fused(): pl.pallas_call(functools.partial(fused_kernel, npts, ncb), out_shape=(plt...  68.8 us
    pallas_call x1, Pallas kernels, finish(): pl.pallas_call(finish_kernel, out_shape=(jax.ShapeDtypeStruct(new_one.sha...  1.67 us

profile of v3, /device:TPU:0, one launch (start us, length us, event | category | flops | bytes accessed | tf_op | source)
XLA Modules:
  0.0 71.1 jit_solution(11217563084483192089)
XLA Ops:
  0.6 68.8 %shard_map.76 = (bf16[512,768]{1,0:T(8,128)(2,1)S(1)}, bf16[512,768]{1,0:T(8,128)(2,1)S(1)}, f32[2,1,128]{2,1,0:T(1,128)S(1)}) custom-call(bf16[2048,768]{1,0:T(8,128)(2,1)} %points_in.1, s32[1,2048]{1,0:T(1,128)} %bitcast.2, s32[1,2048]{1,0:T(1,128)} %bitcast.3, bf16[512,768]{1,0:T(8,128)(2,1)} %cent_one_in.1, bf16[512,768]{1,0:T(8,128)(2,1)} %cent_two_in.1), custom_call_target="tpu_custom_call" | custom-call | tf_op jit(solution)/shard_map/pallas_call | solution.py:489
  69.4 1.7 %shard_map.77 = (bf16[512,768]{1,0:T(8,128)(2,1)}, bf16[512,768]{1,0:T(8,128)(2,1)}, f32[2]{0:T(128)}) custom-call(bf16[512,768]{1,0:T(8,128)(2,1)S(1)} %get-tuple-element.6.one_in, bf16[512,768]{1,0:T(8,128)(2,1)S(1)} %get-tuple-element.7.two_in, f32[2,1,128]{2,1,0:T(1,128)S(1)} %get-tuple-element.8.total_in), custom_call_target="tpu_custom_call" | custom-call | tf_op jit(solution)/shard_map/pallas_call | solution.py:465
